TPU v7x, 32 devices: a whole 2x2x4 slice. The times are simulated.
32 devices in a mesh: dp: 8 (over z, y), mp: 4 (over x, core).
Axes of the slice: x: 2, y: 2, z: 4, core: 2. Of those that a mesh axis runs over, the one named last changes fastest.
Arguments:
- prefix_hidden: bfloat16 [32, 1024, 2048], P(('dp', 'mp')), may hold values from -6 to 6
- prefix_len: int32 [32], P('dp'), may hold values from 256 to 1024
- actions: float32 [32, 50, 32], P('dp'), may hold values from -6 to 6
- noise: float32 [32, 50, 32], P('dp'), may hold values from -6 to 6
- time_index: int32 [32], P('dp'), may hold values from 0 to 999
- prefix_gain: float32 [2048], replicated, may hold values from 0.25 to 1.75
- key_weight: bfloat16 [2048, 256], P('dp'), may hold values from -0.125 to 0.125
- value_weight: bfloat16 [2048, 256], P('dp'), may hold values from -0.125 to 0.125
- action_in: bfloat16 [32, 1024], replicated, may hold values from -1 to 1
- attn_gain: float32 [1024], replicated, may hold values from 0.25 to 1.75
- query_w: bfloat16 [1024, 2048], P('dp', 'mp'), may hold values from -0.1875 to 0.1875
- akey_w: bfloat16 [1024, 256], P('dp'), may hold values from -0.1875 to 0.1875
- avalue_w: bfloat16 [1024, 256], P('dp'), may hold values from -0.1875 to 0.1875
- out_w: bfloat16 [2048, 1024], P('mp', 'dp'), may hold values from -0.125 to 0.125
- mlp_gain: float32 [1024], replicated, may hold values from 0.25 to 1.75
- gate_w: bfloat16 [1024, 4096], P('dp', 'mp'), may hold values from -0.1875 to 0.1875
- up_w: bfloat16 [1024, 4096], P('dp', 'mp'), may hold values from -0.1875 to 0.1875
- down_w: bfloat16 [4096, 1024], P('mp', 'dp'), may hold values from -0.09375 to 0.09375
- final_gain: float32 [1024], replicated, may hold values from 0.25 to 1.75
- head_w: bfloat16 [1024, 32], replicated, may hold values from -0.1875 to 0.1875
Outputs:
- velocity: float32 [32, 50, 32], P(('dp', 'mp'))
- ep_loss: float32 [32], P(('dp', 'mp'))
Inputs may be any that keep to these rules, and one draw needn't show every extreme that they name: `prefix_len`: prefix positions at or above an episode's length are padding that no output reads.
All inputs are finite; a program needn't handle non-finite values.
Results may differ from a plain program's by a relative error of at most 0.009.
Values may be sent and summed in bfloat16 or wider, within the bound.
No kernel may reach another device: no remote copies, remote signals or barrier semaphores. Data moves between devices by JAX's collectives and lax.ppermute only.
A program may use at most 64 MiB of HBM per device.

v0:
```python
import math
import jax
import jax.numpy as jnp
from jax import lax
from jax.sharding import PartitionSpec as P

TSTEPS = 1000


def rms(values, gain):
    return values * lax.rsqrt(jnp.mean(values * values, axis=-1, keepdims=True) + 1e-06) * gain


def time_embed(times, width):
    half = width // 2
    steps = jnp.arange(half, dtype=jnp.float32)
    period = 0.004 * jnp.power(jnp.float32(1000.0), steps / (half - 1))
    angle = times[:, None] * (2.0 * math.pi) / period[None, :]
    return jnp.concatenate([jnp.sin(angle), jnp.cos(angle)], axis=-1)


def attend(query, pkeys, pvals, akeys, avals, lengths):
    live = jnp.arange(pkeys.shape[1], dtype=jnp.int32)[None, :] < lengths[:, None]
    scores = jnp.einsum("erd,epd->erp", query, pkeys, preferred_element_type=jnp.float32)
    probs = jnp.where(live[:, None, :], jnp.exp(scores), 0.0)
    action_scores = jnp.einsum("erd,ecd->erc", query, akeys, preferred_element_type=jnp.float32)
    action_probs = jnp.exp(action_scores)
    denom = jnp.sum(probs, axis=-1) + jnp.sum(action_probs, axis=-1)
    weighted = jnp.einsum(
        "erp,epd->erd", probs.astype(jnp.bfloat16), pvals, preferred_element_type=jnp.float32
    )
    weighted = weighted + jnp.einsum(
        "erc,ecd->erd", action_probs.astype(jnp.bfloat16), avals, preferred_element_type=jnp.float32
    )
    return (weighted / denom[:, :, None]).astype(jnp.bfloat16)


def on_device(
    prefix_hidden,
    prefix_len,
    actions,
    noise,
    time_index,
    prefix_gain,
    key_weight,
    value_weight,
    action_in,
    attn_gain,
    query_w,
    akey_w,
    avalue_w,
    out_w,
    mlp_gain,
    gate_w,
    up_w,
    down_w,
    final_gain,
    head_w,
):
    own_eps, positions, width = prefix_hidden.shape
    group_eps, span, adim = actions.shape
    expert = action_in.shape[1]
    head_size = key_weight.shape[1]
    local_heads = query_w.shape[1] // head_size
    rows_total = group_eps * span
    own_rows = own_eps * span
    member = lax.axis_index("mp")
    first_row = member * own_rows
    first_ep = member * own_eps
    times = (time_index.astype(jnp.float32) + 0.5) / TSTEPS
    x_t = times[:, None, None] * noise + (1.0 - times)[:, None, None] * actions
    target = noise - actions
    x_in = x_t.reshape(rows_total, adim).astype(jnp.bfloat16)
    temb = time_embed(times, expert)
    h0 = (
        jnp.dot(x_in, action_in, preferred_element_type=jnp.float32).reshape(
            group_eps, span, expert
        )
        + temb[:, None, :]
    )
    h0 = h0.reshape(rows_total, expert)
    key_full, value_full = (
        lax.all_gather(key_weight, "dp", axis=0, tiled=True),
        lax.all_gather(value_weight, "dp", axis=0, tiled=True),
    )
    prefix_normed = rms(
        prefix_hidden.reshape(own_eps * positions, width).astype(jnp.float32), prefix_gain
    ).astype(jnp.bfloat16)
    pkeys = (
        jnp.dot(prefix_normed, key_full, preferred_element_type=jnp.float32)
        .astype(jnp.bfloat16)
        .reshape(own_eps, positions, head_size)
    )
    pvals = (
        jnp.dot(prefix_normed, value_full, preferred_element_type=jnp.float32)
        .astype(jnp.bfloat16)
        .reshape(own_eps, positions, head_size)
    )
    normed = rms(h0, attn_gain).astype(jnp.bfloat16)
    query_full, akey_full, avalue_full = (
        lax.all_gather(query_w, "dp", axis=0, tiled=True),
        lax.all_gather(akey_w, "dp", axis=0, tiled=True),
        lax.all_gather(avalue_w, "dp", axis=0, tiled=True),
    )
    query = (
        jnp.dot(normed, query_full, preferred_element_type=jnp.float32) * head_size ** (-0.5)
    ).astype(jnp.bfloat16)
    akeys = (
        jnp.dot(normed, akey_full, preferred_element_type=jnp.float32)
        .astype(jnp.bfloat16)
        .reshape(group_eps, span, head_size)
    )
    avals = (
        jnp.dot(normed, avalue_full, preferred_element_type=jnp.float32)
        .astype(jnp.bfloat16)
        .reshape(group_eps, span, head_size)
    )
    keys_all, vals_all = (
        lax.all_gather(pkeys, "mp", axis=0, tiled=True),
        lax.all_gather(pvals, "mp", axis=0, tiled=True),
    )
    attn = attend(
        query.reshape(group_eps, span * local_heads, head_size),
        keys_all,
        vals_all,
        akeys,
        avals,
        prefix_len,
    )
    attn = attn.reshape(rows_total, local_heads * head_size)
    out_full = lax.all_gather(out_w, "dp", axis=1, tiled=True)
    gate_full, up_full = (
        lax.all_gather(gate_w, "dp", axis=0, tiled=True),
        lax.all_gather(up_w, "dp", axis=0, tiled=True),
    )
    down_full = lax.all_gather(down_w, "dp", axis=1, tiled=True)
    h0_own = lax.dynamic_slice_in_dim(h0, first_row, own_rows, 0)
    h1 = h0_own + lax.psum_scatter(
        jnp.dot(attn, out_full, preferred_element_type=jnp.float32).astype(jnp.bfloat16),
        "mp",
        scatter_dimension=0,
        tiled=True,
    ).astype(jnp.float32)
    mixed_own = rms(h1, mlp_gain).astype(jnp.bfloat16)
    mixed = lax.all_gather(mixed_own, "mp", axis=0, tiled=True)
    gate = jnp.dot(mixed, gate_full, preferred_element_type=jnp.float32)
    upper = jnp.dot(mixed, up_full, preferred_element_type=jnp.float32)
    hidden = (jax.nn.gelu(gate, approximate=True) * upper).astype(jnp.bfloat16)
    h2 = h1 + lax.psum_scatter(
        jnp.dot(hidden, down_full, preferred_element_type=jnp.float32).astype(jnp.bfloat16),
        "mp",
        scatter_dimension=0,
        tiled=True,
    ).astype(jnp.float32)
    final = rms(h2, final_gain).astype(jnp.bfloat16)
    velocity = jnp.dot(final, head_w, preferred_element_type=jnp.float32).reshape(
        own_eps, span, adim
    )
    own_target = lax.dynamic_slice_in_dim(target, first_ep, own_eps, 0)
    diff = velocity - own_target
    ep_loss = jnp.mean(diff * diff, axis=(1, 2))
    return (velocity, ep_loss)


def solution(mesh):
    in_specs = (
        P(("dp", "mp"), None, None),
        P("dp"),
        P("dp", None, None),
        P("dp", None, None),
        P("dp"),
        P(),
        P("dp", None),
        P("dp", None),
        P(),
        P(),
        P("dp", "mp"),
        P("dp", None),
        P("dp", None),
        P("mp", "dp"),
        P(),
        P("dp", "mp"),
        P("dp", "mp"),
        P("mp", "dp"),
        P(),
        P(),
    )
    out_specs = (P(("dp", "mp"), None, None), P(("dp", "mp")))
    return jax.shard_map(
        on_device, mesh=mesh, in_specs=in_specs, out_specs=out_specs, check_vma=False
    )
```

profile of v0, /device:TPU:6, one launch (start us, length us, event | category | flops | bytes accessed | tf_op | source)
XLA Modules:
  0.0 404.9 jit_solution(4263375516487390356)
XLA Ops:
  7.2 0.7 all-gather.15.cloned.1.call-update
  8.0 0.7 all-gather.17.cloned.1.call-update
  8.7 0.7 all-gather.13.cloned.1.call-update
  9.5 3.1 fusion.2
  12.5 38.1 %all-gather.15.cloned.1.call-done = bf16[2048,256]{1,0:T(8,128)(2,1)} async-done(((bf16[256,256]{1,0:T(8,128)(2,1)}), bf16[2048,256]{1,0:T(8,128)(2,1)}) %all-gather.15.cloned.1.call-update) | async-done | bytes 1048592 | tf_op jit(solution)/shard_map/all_gather | solution.py:83
  50.7 4.6 %convolution_convert_fusion.1 = bf16[1024,256]{1,0:T(8,128)(2,1)} fusion(bf16[2048,256]{1,0:T(8,128)(2,1)} %all-gather.15.cloned.1.call-done, bf16[1,1024,2048]{2,1,0:T(8,128)(2,1)} %param.20, f32[2048]{0:T(1024)S(1)} %copy-done.12, f32[1024]{0:T(1024)S(1)} %add_rsqrt_fusion), kind=kOutput, calls=%fused_computation.9 | convolution fusion | flops 1082392576 | bytes 5779456 | tf_op jit(solution)/shard_map/dot_general | solution.py:90
  55.4 36.4 %all-gather.17.cloned.1.call-done = bf16[2048,256]{1,0:T(8,128)(2,1)} async-done(((bf16[256,256]{1,0:T(8,128)(2,1)}), bf16[2048,256]{1,0:T(8,128)(2,1)}) %all-gather.17.cloned.1.call-update) | async-done | bytes 1048592 | tf_op jit(solution)/shard_map/all_gather | solution.py:84
  91.8 4.6 %convolution_convert_fusion = bf16[1024,256]{1,0:T(8,128)(2,1)} fusion(bf16[2048,256]{1,0:T(8,128)(2,1)} %all-gather.17.cloned.1.call-done, bf16[1,1024,2048]{2,1,0:T(8,128)(2,1)} %param.20, f32[2048]{0:T(1024)S(1)} %copy-done.12, f32[1024]{0:T(1024)S(1)} %add_rsqrt_fusion), kind=kOutput, calls=%fused_computation.8 | convolution fusion | flops 1082392576 | bytes 5779456 | tf_op jit(solution)/shard_map/dot_general | solution.py:95
  96.5 0.5 all-gather.19.cloned.1.call-update
  97.1 0.7 all-gather.21.cloned.1.call-update
  97.8 0.7 all-gather.23.cloned.1.call-update
  98.6 0.7 all-gather.25.cloned.1.call-update
  99.3 0.1 fusion.38
  99.5 0.5 multiply_reduce_fusion
  100.0 0.1 reshape.115
  100.2 30.9 %all_gather.41 = bf16[1024,256]{1,0:T(8,128)(2,1)S(1)} all-gather(bf16[128,256]{1,0:T(8,128)(2,1)S(1)} %copy-done.3), channel_id=1, replica_groups=mesh['dp'=8,'mp'=4] {'dp'}, dimensions={0}, use_global_device_ids=true | all-gather | bytes 589824 | tf_op jit(solution)/shard_map/all_gather | solution.py:102
  131.1 0.1 multiply_convert_fusion
  131.2 0.3 convolution_convert_fusion.5
  131.6 31.5 %all_gather.42 = bf16[1024,256]{1,0:T(8,128)(2,1)S(1)} all-gather(bf16[128,256]{1,0:T(8,128)(2,1)S(1)} %copy-done.4), channel_id=1, replica_groups=mesh['dp'=8,'mp'=4] {'dp'}, dimensions={0}, use_global_device_ids=true | all-gather | bytes 589824 | tf_op jit(solution)/shard_map/all_gather | solution.py:103
  163.1 0.3 convolution_convert_fusion.4
  163.5 1.6 fusion.10
  165.2 0.2 fusion.46
  165.5 2.5 fusion.45
  168.0 14.4 %all-gather.29.cloned.1.call-done = bf16[4096,256]{1,0:T(8,128)(2,1)} async-done(((bf16[1024,256]{1,0:T(8,128)(2,1)}), bf16[4096,256]{1,0:T(8,128)(2,1)}) %all-gather.29.cloned.1.call-update) | async-done | bytes 2097168 | tf_op jit(solution)/shard_map/all_gather | solution.py:120
  182.4 2.0 fusion.11
  184.5 0.3 fusion.9
  184.8 39.4 %all-gather.19.cloned.1.call-done = bf16[512,1024]{1,0:T(8,128)(2,1)} async-done(((bf16[512,128]{1,0:T(8,128)(2,1)}), bf16[512,1024]{1,0:T(8,128)(2,1)}) %all-gather.19.cloned.1.call-update) | async-done | bytes 1048592 | tf_op jit(solution)/shard_map/all_gather | solution.py:131
  224.2 1.6 convolution_convert_fusion.3
  225.8 10.1 %fusion = bf16[56,1024]{1,0:T(8,128)(2,1)S(1)} fusion(bf16[200,1024]{1,0:T(8,128)(2,1)S(1)} %convolution_convert_fusion.3), kind=kCustom, calls=%all-reduce-scatter | all-reduce-scatter fusion | flops 229377 | bytes 524800
  236.0 1.9 collective-permute-start
  237.9 0.6 dynamic-slice.6
  239.1 2.2 collective-permute-done
  241.4 0.2 concatenate.4
  241.6 0.2 multiply_reduce_fusion.2
  241.8 0.1 fusion.25
  241.9 6.3 %all-gather.2 = bf16[4,50,1024]{2,1,0:T(8,128)(2,1)S(1)} all-gather(bf16[1,50,1024]{2,1,0:T(8,128)(2,1)S(1)} %fusion.25), channel_id=1, replica_groups=mesh['dp'=8,'mp'=4] {'mp'}, dimensions={0}, use_global_device_ids=true | all-gather | bytes 512000 | tf_op jit(solution)/shard_map/all_gather | solution.py:145
  248.2 0.1 reshape.127
  248.3 25.8 %all-gather.21.cloned.1.call-done = bf16[1024,1024]{1,0:T(8,128)(2,1)} async-done(((bf16[128,1024]{1,0:T(8,128)(2,1)}), bf16[1024,1024]{1,0:T(8,128)(2,1)}) %all-gather.21.cloned.1.call-update) | async-done | bytes 2097168 | tf_op jit(solution)/shard_map/all_gather | solution.py:133
  274.1 2.2 fusion.47
  276.3 47.6 %all-gather.23.cloned.1.call-done = bf16[1024,1024]{1,0:T(8,128)(2,1)} async-done(((bf16[128,1024]{1,0:T(8,128)(2,1)}), bf16[1024,1024]{1,0:T(8,128)(2,1)}) %all-gather.23.cloned.1.call-update) | async-done | bytes 2097168 | tf_op jit(solution)/shard_map/all_gather | solution.py:134
  323.8 51.9 %all-gather.25.cloned.1.call-done = bf16[1024,1024]{1,0:T(8,128)(2,1)} async-done(((bf16[1024,128]{1,0:T(8,128)(2,1)}), bf16[1024,1024]{1,0:T(8,128)(2,1)}) %all-gather.25.cloned.1.call-update) | async-done | bytes 2097168 | tf_op jit(solution)/shard_map/all_gather | solution.py:136
  375.7 3.3 convolution_convert_fusion.2
  379.0 10.2 %fusion.1 = bf16[56,1024]{1,0:T(8,128)(2,1)S(1)} fusion(bf16[200,1024]{1,0:T(8,128)(2,1)S(1)} %convolution_convert_fusion.2), kind=kCustom, calls=%all-reduce-scatter.1 | all-reduce-scatter fusion | flops 229377 | bytes 524800
  389.3 1.9 collective-permute-start.1
  391.2 3.5 collective-permute-done.1
  394.7 0.2 concatenate.5
  394.9 0.2 multiply_reduce_fusion.1
  395.1 1.5 fusion.35
  (55 shorter events, 1.0 us)
Async XLA Ops:
  7.2 92.3 %copy-start = (bf16[32,1024]{1,0:T(8,128)(2,1)S(1)}, bf16[32,1024]{1,0:T(8,128)(2,1)}, u32[]{:S(2)}) copy-start(bf16[32,1024]{1,0:T(8,128)(2,1)} %param.28) | copy-start | bytes 196612
  7.2 43.5 %all-gather.15.cloned.1.call-start = ((), (), s32[]{:S(2)}) async-start(), calls=%async_computation.1 | async-start | bytes 1179648 | tf_op jit(solution)/shard_map/all_gather | solution.py:83
  7.9 83.9 %all-gather.17.cloned.1.call-start = ((), (), s32[]{:S(2)}) async-start(), calls=%async_computation.2 | async-start | bytes 1179648 | tf_op jit(solution)/shard_map/all_gather | solution.py:84
  8.7 154.9 %all-gather.13.cloned.1.call-start = ((), (), s32[]{:S(2)}) async-start(), calls=%async_computation | async-start | bytes 1179648 | tf_op jit(solution)/shard_map/all_gather | solution.py:101
  9.4 41.3 %copy-start.12 = (f32[2048]{0:T(1024)S(1)}, f32[2048]{0:T(1024)}, u32[]{:S(2)}) copy-start(f32[2048]{0:T(1024)} %param.25) | copy-start | bytes 24580
  9.4 156.1 %all-gather.27.cloned.1.call-start = ((), (), s32[]{:S(2)}) async-start(), calls=%async_computation.7 | async-start | bytes 2621440 | tf_op jit(solution)/shard_map/all_gather | solution.py:119
  55.4 43.9 %copy-start.11 = (s32[4]{0:T(128)S(1)}, s32[4]{0:T(128)}, u32[]{:S(2)}) copy-start(s32[4]{0:T(128)} %param.24) | copy-start | bytes 52
  55.4 44.1 %copy-start.1 = (f32[4,50,32]{1,2,0:T(8,128)S(1)}, f32[4,50,32]{1,2,0:T(8,128)}, u32[]{:S(2)}) copy-start(f32[4,50,32]{1,2,0:T(8,128)} %param.22) | copy-start | bytes 76804
  55.4 44.1 %copy-start.2 = (f32[4,50,32]{1,2,0:T(8,128)S(1)}, f32[4,50,32]{1,2,0:T(8,128)}, u32[]{:S(2)}) copy-start(f32[4,50,32]{1,2,0:T(8,128)} %param.23) | copy-start | bytes 76804
  55.4 127.0 %all-gather.29.cloned.1.call-start = ((), (), s32[]{:S(2)}) async-start(), calls=%async_computation.8 | async-start | bytes 2621440 | tf_op jit(solution)/shard_map/all_gather | solution.py:120
  96.4 3.8 copy-start.3
  96.5 127.8 %all-gather.19.cloned.1.call-start = ((), (), s32[]{:S(2)}) async-start(), calls=%async_computation.3 | async-start | bytes 1179648 | tf_op jit(solution)/shard_map/all_gather | solution.py:131
  97.0 34.1 %copy-start.6 = (f32[1024]{0:T(1024)S(1)}, f32[1024]{0:T(1024)}, u32[]{:S(2)}) copy-start(f32[1024]{0:T(1024)} %param.29) | copy-start | bytes 12292
  97.0 177.0 %all-gather.21.cloned.1.call-start = ((), (), s32[]{:S(2)}) async-start(), calls=%async_computation.4 | async-start | bytes 2359296 | tf_op jit(solution)/shard_map/all_gather | solution.py:133
  97.8 226.0 %all-gather.23.cloned.1.call-start = ((), (), s32[]{:S(2)}) async-start(), calls=%async_computation.5 | async-start | bytes 2359296 | tf_op jit(solution)/shard_map/all_gather | solution.py:134
  98.5 277.1 %all-gather.25.cloned.1.call-start = ((), (), s32[]{:S(2)}) async-start(), calls=%async_computation.6 | async-start | bytes 2359296 | tf_op jit(solution)/shard_map/all_gather | solution.py:136
  100.0 31.6 %copy-start.4 = (bf16[128,256]{1,0:T(8,128)(2,1)S(1)}, bf16[128,256]{1,0:T(8,128)(2,1)}, u32[]{:S(2)}) copy-start(bf16[128,256]{1,0:T(8,128)(2,1)} %param.32) | copy-start | bytes 196612
  131.1 32.4 %copy-start.9 = (s32[4]{0:T(128)S(1)}, s32[4]{0:T(128)}, u32[]{:S(2)}) copy-start(s32[4]{0:T(128)} %param.21) | copy-start | bytes 52
  184.5 53.4 %copy-start.10 = (u32[32]{0:T(128)S(1)}, u32[32]{0:T(128)}, u32[]{:S(2)}) copy-start(u32[32]{0:T(128)} %constant.63) | copy-start | bytes 388
  184.7 57.0 %copy-start.7 = (f32[1024]{0:T(1024)S(1)}, f32[1024]{0:T(1024)}, u32[]{:S(2)}) copy-start(f32[1024]{0:T(1024)} %param.34) | copy-start | bytes 12292
  236.0 5.4 %collective-permute-start = (bf16[18,1024]{1,0:T(8,128)(2,1)S(1)}, bf16[18,1024]{1,0:T(8,128)(2,1)S(1)}, u32[]{:S(2)}, u32[]{:S(2)}) collective-permute-start(bf16[18,1024]{1,0:T(8,128)(2,1)S(1)} %slice), channel_id=1, source_target_pairs={{0,1},{1,2},{2,3},{4,5},{5,6},{6,7},{8,9},{9,10},{10,11},{12,13},{... | collective-permute-start | bytes 110600
  276.2 118.9 %copy-start.5 = (bf16[1024,32]{0,1:T(8,128)(2,1)S(1)}, bf16[1024,32]{0,1:T(8,128)(2,1)}, u32[]{:S(2)}) copy-start(bf16[1024,32]{0,1:T(8,128)(2,1)} %param.39) | copy-start | bytes 196612
  276.3 118.9 %copy-start.8 = (f32[1024]{0:T(1024)S(1)}, f32[1024]{0:T(1024)}, u32[]{:S(2)}) copy-start(f32[1024]{0:T(1024)} %param.38) | copy-start | bytes 12292
  389.3 5.4 %collective-permute-start.1 = (bf16[18,1024]{1,0:T(8,128)(2,1)S(1)}, bf16[18,1024]{1,0:T(8,128)(2,1)S(1)}, u32[]{:S(2)}, u32[]{:S(2)}) collective-permute-start(bf16[18,1024]{1,0:T(8,128)(2,1)S(1)} %slice.1), channel_id=1, source_target_pairs={{0,1},{1,2},{2,3},{4,5},{5,6},{6,7},{8,9},{9,10},{10,11},{12,13},{... | collective-permute-start | bytes 110600
Sparse Core Ops, SparseCore 0:
  10.1 40.5 all-gather.14
  52.8 38.9 all-gather.16
  94.0 41.6 all-gather.12
  137.0 21.2 all-gather.26
  159.8 22.5 all-gather.28
  184.3 39.8 all-gather.18
  226.3 47.6 all-gather.20
  276.2 47.6 all-gather.22
  325.9 49.7 all-gather.24
where the time goes:
time: 405 us
  waiting for transfers between devices  264 us (65%)
  blocking collectives  89.1 us (22%)
  matrix products  25.5 us (6%)
  between operations  16.7 us (4%)
  starting transfers between devices  4.19 us (1%)
    all_gather x1, waiting for transfers between devices, on_device(): down_full = lax.all_gather(down_w, 'dp', axis=1, tiled=True)  51.9 us
    all_gather x1, waiting for transfers between devices, on_device(): lax.all_gather(up_w, 'dp', axis=0, tiled=True)  47.6 us
    all_gather x1, waiting for transfers between devices, on_device(): out_full = lax.all_gather(out_w, 'dp', axis=1, tiled=True)  39.4 us
    all_gather x1, waiting for transfers between devices, on_device(): lax.all_gather(key_weight, 'dp', axis=0, tiled=True)  38.1 us
    all_gather x1, waiting for transfers between devices, on_device(): lax.all_gather(value_weight, 'dp', axis=0, tiled=True)  36.4 us
    all_gather x1, blocking collectives, on_device(): lax.all_gather(avalue_w, 'dp', axis=0, tiled=True)  31.5 us
    all_gather x1, blocking collectives, on_device(): lax.all_gather(akey_w, 'dp', axis=0, tiled=True)  30.9 us
    all_gather x1, waiting for transfers between devices, on_device(): lax.all_gather(gate_w, 'dp', axis=0, tiled=True)  25.8 us
  transfers between devices with their start and end apart: 11, of which 9 were waited for; matrix products, arithmetic and copies ran while one was open for 9% of the time, Pallas kernels for 0%

commit v1 on v0

--- a/solution.py
+++ b/solution.py
@@ -128,7 +128,7 @@
         prefix_len,
     )
     attn = attn.reshape(rows_total, local_heads * head_size)
-    out_full = lax.all_gather(out_w, "dp", axis=1, tiled=True)
+    out_full = jnp.concatenate(lax.all_gather(out_w, "dp"), axis=1)
     gate_full, up_full = (
         lax.all_gather(gate_w, "dp", axis=0, tiled=True),
         lax.all_gather(up_w, "dp", axis=0, tiled=True),

time: 405 us -> 407 us (level)
    all_gather x1, waiting for transfers between devices: 39.4 us -> 12.2 us  [on_device(): out_full = jnp.concatenate(lax.all_gather(out_w, 'dp'), axis=1)]
    all_gather x1, waiting for transfers between devices: 0.02 us -> 21 us  [on_device(): lax.all_gather(pkeys, 'mp', axis=0, tiled=True)]
    all_gather x1, waiting for transfers between devices: 14.4 us -> 21.5 us  [on_device(): lax.all_gather(pvals, 'mp', axis=0, tiled=True)]
  transfers between devices with their start and end apart: 11 -> 11, of which waited for: 9 -> 10; matrix products, arithmetic and copies ran while one was open for 9% -> 9% of each run, Pallas kernels for 0% -> 0%
where the time goes in v1:
time: 407 us; the launch traced here: 406 us
  waiting for transfers between devices  264 us (65%)
  blocking collectives  90.1 us (22%)
  matrix products  24.3 us (6%)
  between operations  16.7 us (4%)
  starting transfers between devices  4.19 us (1%)
    all_gather x1, waiting for transfers between devices, on_device(): down_full = lax.all_gather(down_w, 'dp', axis=1, tiled=True)  51.9 us
    all_gather x1, waiting for transfers between devices, on_device(): lax.all_gather(up_w, 'dp', axis=0, tiled=True)  47.6 us
    all_gather x1, waiting for transfers between devices, on_device(): lax.all_gather(key_weight, 'dp', axis=0, tiled=True)  37.6 us
    all_gather x1, waiting for transfers between devices, on_device(): lax.all_gather(value_weight, 'dp', axis=0, tiled=True)  36.4 us
    all_gather x1, blocking collectives, on_device(): lax.all_gather(avalue_w, 'dp', axis=0, tiled=True)  31.8 us
    all_gather x1, blocking collectives, on_device(): lax.all_gather(akey_w, 'dp', axis=0, tiled=True)  31.1 us
    all_gather x1, waiting for transfers between devices, on_device(): lax.all_gather(gate_w, 'dp', axis=0, tiled=True)  25.3 us
    all_gather x1, waiting for transfers between devices, on_device(): lax.all_gather(pvals, 'mp', axis=0, tiled=True)  21.5 us
  transfers between devices with their start and end apart: 11, of which 10 were waited for; matrix products, arithmetic and copies ran while one was open for 9% of the time, Pallas kernels for 0%

profile of v1, /device:TPU:6, one launch (start us, length us, event | category | flops | bytes accessed | tf_op | source)
XLA Modules:
  0.0 406.2 jit_solution(4182927624271056328)
XLA Ops:
  7.2 0.7 all-gather.16.cloned.1.call-update
  8.0 0.7 all-gather.18.cloned.1.call-update
  8.7 0.7 all-gather.14.cloned.1.call-update
  9.4 0.5 all-gather.30.cloned.1.call-update
  10.0 3.1 fusion.2
  13.1 37.6 %all-gather.16.cloned.1.call-done = bf16[2048,256]{1,0:T(8,128)(2,1)} async-done(((bf16[256,256]{1,0:T(8,128)(2,1)}), bf16[2048,256]{1,0:T(8,128)(2,1)}) %all-gather.16.cloned.1.call-update) | async-done | bytes 1048592 | tf_op jit(solution)/shard_map/all_gather | solution.py:83
  50.7 4.6 %convolution_convert_fusion.1 = bf16[1024,256]{1,0:T(8,128)(2,1)} fusion(bf16[2048,256]{1,0:T(8,128)(2,1)} %all-gather.16.cloned.1.call-done, bf16[1,1024,2048]{2,1,0:T(8,128)(2,1)} %param.20, f32[2048]{0:T(1024)S(1)} %copy-done.12, f32[1024]{0:T(1024)S(1)} %add_rsqrt_fusion), kind=kOutput, calls=%fused_computation.9 | convolution fusion | flops 1082392576 | bytes 5779456 | tf_op jit(solution)/shard_map/dot_general | solution.py:90
  55.4 36.4 %all-gather.18.cloned.1.call-done = bf16[2048,256]{1,0:T(8,128)(2,1)} async-done(((bf16[256,256]{1,0:T(8,128)(2,1)}), bf16[2048,256]{1,0:T(8,128)(2,1)}) %all-gather.18.cloned.1.call-update) | async-done | bytes 1048592 | tf_op jit(solution)/shard_map/all_gather | solution.py:84
  91.8 4.6 %convolution_convert_fusion = bf16[1024,256]{1,0:T(8,128)(2,1)} fusion(bf16[2048,256]{1,0:T(8,128)(2,1)} %all-gather.18.cloned.1.call-done, bf16[1,1024,2048]{2,1,0:T(8,128)(2,1)} %param.20, f32[2048]{0:T(1024)S(1)} %copy-done.12, f32[1024]{0:T(1024)S(1)} %add_rsqrt_fusion), kind=kOutput, calls=%fused_computation.8 | convolution fusion | flops 1082392576 | bytes 5779456 | tf_op jit(solution)/shard_map/dot_general | solution.py:95
  96.5 0.7 all-gather.20.cloned.1.call-update
  97.3 0.7 all-gather.22.cloned.1.call-update
  98.0 0.7 all-gather.24.cloned.1.call-update
  98.7 0.1 fusion.38
  98.9 0.5 multiply_reduce_fusion
  99.6 31.1 %all_gather.44 = bf16[1024,256]{1,0:T(8,128)(2,1)S(1)} all-gather(bf16[128,256]{1,0:T(8,128)(2,1)S(1)} %copy-done.3), channel_id=1, replica_groups=mesh['dp'=8,'mp'=4] {'dp'}, dimensions={0}, use_global_device_ids=true | all-gather | bytes 589824 | tf_op jit(solution)/shard_map/all_gather | solution.py:102
  130.7 0.1 multiply_convert_fusion
  130.8 0.3 convolution_convert_fusion.5
  131.2 31.8 %all_gather.45 = bf16[1024,256]{1,0:T(8,128)(2,1)S(1)} all-gather(bf16[128,256]{1,0:T(8,128)(2,1)S(1)} %copy-done.4), channel_id=1, replica_groups=mesh['dp'=8,'mp'=4] {'dp'}, dimensions={0}, use_global_device_ids=true | all-gather | bytes 589824 | tf_op jit(solution)/shard_map/all_gather | solution.py:103
  163.0 0.3 convolution_convert_fusion.4
  163.4 1.6 fusion.10
  165.1 12.2 %all-gather.30.cloned.1.call-done = bf16[4096,128]{1,0:T(8,128)(2,1)} async-done(((bf16[512,128]{1,0:T(8,128)(2,1)}), bf16[4096,128]{1,0:T(8,128)(2,1)}) %all-gather.30.cloned.1.call-update) | async-done | bytes 1048592 | tf_op jit(solution)/shard_map/all_gather | solution.py:131
  177.4 1.5 copy.23
  178.8 0.2 fusion.46
  179.1 21.0 %all-gather.26.cloned.1.call-done = bf16[4096,256]{1,0:T(8,128)(2,1)} async-done(((bf16[1024,256]{1,0:T(8,128)(2,1)}), bf16[4096,256]{1,0:T(8,128)(2,1)}) %all-gather.26.cloned.1.call-update) | async-done | bytes 2097168 | tf_op jit(solution)/shard_map/all_gather | solution.py:119
  200.1 2.5 fusion.45
  202.5 21.5 %all-gather.28.cloned.1.call-done = bf16[4096,256]{1,0:T(8,128)(2,1)} async-done(((bf16[1024,256]{1,0:T(8,128)(2,1)}), bf16[4096,256]{1,0:T(8,128)(2,1)}) %all-gather.28.cloned.1.call-update) | async-done | bytes 2097168 | tf_op jit(solution)/shard_map/all_gather | solution.py:120
  224.1 2.0 fusion.11
  226.1 0.3 fusion.9
  226.5 0.5 convolution_convert_fusion.3
  227.0 10.6 %fusion = bf16[56,1024]{1,0:T(8,128)(2,1)S(1)} fusion(bf16[200,1024]{1,0:T(8,128)(2,1)S(1)} %convolution_convert_fusion.3), kind=kCustom, calls=%all-reduce-scatter | all-reduce-scatter fusion | flops 229377 | bytes 524800
  237.7 1.9 collective-permute-start
  239.6 0.6 dynamic-slice.6
  240.9 2.2 collective-permute-done
  243.1 0.2 concatenate.4
  243.3 0.2 multiply_reduce_fusion.2
  243.6 6.3 %all-gather.3 = bf16[4,50,1024]{2,1,0:T(8,128)(2,1)S(1)} all-gather(bf16[1,50,1024]{2,1,0:T(8,128)(2,1)S(1)} %fusion.25), channel_id=1, replica_groups=mesh['dp'=8,'mp'=4] {'mp'}, dimensions={0}, use_global_device_ids=true | all-gather | bytes 512000 | tf_op jit(solution)/shard_map/all_gather | solution.py:145
  249.9 0.1 reshape.136
  250.0 25.3 %all-gather.20.cloned.1.call-done = bf16[1024,1024]{1,0:T(8,128)(2,1)} async-done(((bf16[128,1024]{1,0:T(8,128)(2,1)}), bf16[1024,1024]{1,0:T(8,128)(2,1)}) %all-gather.20.cloned.1.call-update) | async-done | bytes 2097168 | tf_op jit(solution)/shard_map/all_gather | solution.py:133
  275.3 2.2 fusion.47
  277.5 47.6 %all-gather.22.cloned.1.call-done = bf16[1024,1024]{1,0:T(8,128)(2,1)} async-done(((bf16[128,1024]{1,0:T(8,128)(2,1)}), bf16[1024,1024]{1,0:T(8,128)(2,1)}) %all-gather.22.cloned.1.call-update) | async-done | bytes 2097168 | tf_op jit(solution)/shard_map/all_gather | solution.py:134
  325.1 51.9 %all-gather.24.cloned.1.call-done = bf16[1024,1024]{1,0:T(8,128)(2,1)} async-done(((bf16[1024,128]{1,0:T(8,128)(2,1)}), bf16[1024,1024]{1,0:T(8,128)(2,1)}) %all-gather.24.cloned.1.call-update) | async-done | bytes 2097168 | tf_op jit(solution)/shard_map/all_gather | solution.py:136
  377.0 3.3 convolution_convert_fusion.2
  380.3 10.2 %fusion.1 = bf16[56,1024]{1,0:T(8,128)(2,1)S(1)} fusion(bf16[200,1024]{1,0:T(8,128)(2,1)S(1)} %convolution_convert_fusion.2), kind=kCustom, calls=%all-reduce-scatter.1 | all-reduce-scatter fusion | flops 229377 | bytes 524800
  390.6 1.9 collective-permute-start.1
  392.5 3.5 collective-permute-done.1
  396.0 0.2 concatenate.5
  396.2 0.2 multiply_reduce_fusion.1
  396.4 1.5 fusion.35
  (56 shorter events, 1.2 us)
Async XLA Ops:
  7.2 91.7 %copy-start = (bf16[32,1024]{1,0:T(8,128)(2,1)S(1)}, bf16[32,1024]{1,0:T(8,128)(2,1)}, u32[]{:S(2)}) copy-start(bf16[32,1024]{1,0:T(8,128)(2,1)} %param.28) | copy-start | bytes 196612
  7.2 43.5 %all-gather.16.cloned.1.call-start = ((), (), s32[]{:S(2)}) async-start(), calls=%async_computation.1 | async-start | bytes 1179648 | tf_op jit(solution)/shard_map/all_gather | solution.py:83
  7.9 83.9 %all-gather.18.cloned.1.call-start = ((), (), s32[]{:S(2)}) async-start(), calls=%async_computation.2 | async-start | bytes 1179648 | tf_op jit(solution)/shard_map/all_gather | solution.py:84
  8.7 154.7 %all-gather.14.cloned.1.call-start = ((), (), s32[]{:S(2)}) async-start(), calls=%async_computation | async-start | bytes 1179648 | tf_op jit(solution)/shard_map/all_gather | solution.py:101
  9.4 168.0 %all-gather.30.cloned.1.call-start = ((), (), s32[]{:S(2)}) async-start(), calls=%async_computation.8 | async-start | bytes 1179648 | tf_op jit(solution)/shard_map/all_gather | solution.py:131
  10.0 40.7 %copy-start.12 = (f32[2048]{0:T(1024)S(1)}, f32[2048]{0:T(1024)}, u32[]{:S(2)}) copy-start(f32[2048]{0:T(1024)} %param.25) | copy-start | bytes 24580
  10.0 190.1 %all-gather.26.cloned.1.call-start = ((), (), s32[]{:S(2)}) async-start(), calls=%async_computation.6 | async-start | bytes 2621440 | tf_op jit(solution)/shard_map/all_gather | solution.py:119
  55.4 43.4 %copy-start.11 = (s32[4]{0:T(128)S(1)}, s32[4]{0:T(128)}, u32[]{:S(2)}) copy-start(s32[4]{0:T(128)} %param.24) | copy-start | bytes 52
  55.4 43.5 %copy-start.1 = (f32[4,50,32]{1,2,0:T(8,128)S(1)}, f32[4,50,32]{1,2,0:T(8,128)}, u32[]{:S(2)}) copy-start(f32[4,50,32]{1,2,0:T(8,128)} %param.22) | copy-start | bytes 76804
  55.4 43.5 %copy-start.2 = (f32[4,50,32]{1,2,0:T(8,128)S(1)}, f32[4,50,32]{1,2,0:T(8,128)}, u32[]{:S(2)}) copy-start(f32[4,50,32]{1,2,0:T(8,128)} %param.23) | copy-start | bytes 76804
  55.4 168.7 %all-gather.28.cloned.1.call-start = ((), (), s32[]{:S(2)}) async-start(), calls=%async_computation.7 | async-start | bytes 2621440 | tf_op jit(solution)/shard_map/all_gather | solution.py:120
  96.4 3.2 copy-start.3
  96.5 34.2 %copy-start.6 = (f32[1024]{0:T(1024)S(1)}, f32[1024]{0:T(1024)}, u32[]{:S(2)}) copy-start(f32[1024]{0:T(1024)} %param.29) | copy-start | bytes 12292
  96.5 178.9 %all-gather.20.cloned.1.call-start = ((), (), s32[]{:S(2)}) async-start(), calls=%async_computation.3 | async-start | bytes 2359296 | tf_op jit(solution)/shard_map/all_gather | solution.py:133
  97.2 227.9 %all-gather.22.cloned.1.call-start = ((), (), s32[]{:S(2)}) async-start(), calls=%async_computation.4 | async-start | bytes 2359296 | tf_op jit(solution)/shard_map/all_gather | solution.py:134
  98.0 279.0 %all-gather.24.cloned.1.call-start = ((), (), s32[]{:S(2)}) async-start(), calls=%async_computation.5 | async-start | bytes 2359296 | tf_op jit(solution)/shard_map/all_gather | solution.py:136
  99.4 31.8 %copy-start.4 = (bf16[128,256]{1,0:T(8,128)(2,1)S(1)}, bf16[128,256]{1,0:T(8,128)(2,1)}, u32[]{:S(2)}) copy-start(bf16[128,256]{1,0:T(8,128)(2,1)} %param.32) | copy-start | bytes 196612
  130.7 32.6 %copy-start.9 = (s32[4]{0:T(128)S(1)}, s32[4]{0:T(128)}, u32[]{:S(2)}) copy-start(s32[4]{0:T(128)} %param.21) | copy-start | bytes 52
  226.1 13.5 %copy-start.10 = (u32[32]{0:T(128)S(1)}, u32[32]{0:T(128)}, u32[]{:S(2)}) copy-start(u32[32]{0:T(128)} %constant.63) | copy-start | bytes 388
  226.4 17.1 %copy-start.7 = (f32[1024]{0:T(1024)S(1)}, f32[1024]{0:T(1024)}, u32[]{:S(2)}) copy-start(f32[1024]{0:T(1024)} %param.34) | copy-start | bytes 12292
  237.7 5.4 %collective-permute-start = (bf16[18,1024]{1,0:T(8,128)(2,1)S(1)}, bf16[18,1024]{1,0:T(8,128)(2,1)S(1)}, u32[]{:S(2)}, u32[]{:S(2)}) collective-permute-start(bf16[18,1024]{1,0:T(8,128)(2,1)S(1)} %slice), channel_id=1, source_target_pairs={{0,1},{1,2},{2,3},{4,5},{5,6},{6,7},{8,9},{9,10},{10,11},{12,13},{... | collective-permute-start | bytes 110600
  277.5 118.9 %copy-start.5 = (bf16[1024,32]{0,1:T(8,128)(2,1)S(1)}, bf16[1024,32]{0,1:T(8,128)(2,1)}, u32[]{:S(2)}) copy-start(bf16[1024,32]{0,1:T(8,128)(2,1)} %param.39) | copy-start | bytes 196612
  277.5 118.9 %copy-start.8 = (f32[1024]{0:T(1024)S(1)}, f32[1024]{0:T(1024)}, u32[]{:S(2)}) copy-start(f32[1024]{0:T(1024)} %param.38) | copy-start | bytes 12292
  390.6 5.4 %collective-permute-start.1 = (bf16[18,1024]{1,0:T(8,128)(2,1)S(1)}, bf16[18,1024]{1,0:T(8,128)(2,1)S(1)}, u32[]{:S(2)}, u32[]{:S(2)}) collective-permute-start(bf16[18,1024]{1,0:T(8,128)(2,1)S(1)} %slice.1), channel_id=1, source_target_pairs={{0,1},{1,2},{2,3},{4,5},{5,6},{6,7},{8,9},{9,10},{10,11},{12,13},{... | collective-permute-start | bytes 110600
Sparse Core Ops, SparseCore 0:
  10.1 40.5 all-gather.15
  52.8 38.9 all-gather.17
  94.0 41.6 all-gather.13
  137.7 39.6 all-gather.29
  178.8 21.2 all-gather.25
  201.5 22.5 all-gather.27
  226.2 49.0 all-gather.19
  277.4 47.6 all-gather.21
  327.1 49.7 all-gather.23
